TPU v7x, 32 devices: a whole 2x2x4 slice. The times are simulated.
32 devices in a mesh: seq: 8 (over z, x), tensor: 4 (over y, core).
Axes of the slice: x: 2, y: 2, z: 4, core: 2. Of those that a mesh axis runs over, the one named last changes fastest.
Arguments:
- tokens: bfloat16 [4096, 2048], P('seq', 'tensor'), may hold values from -12 to 12
- attn_gain: float32 [2048], replicated, may hold values from 0.1 to 1.9
- w_query: bfloat16 [2048, 2048], P('seq', 'tensor'), as said below
- w_key: bfloat16 [2048, 512], P('seq', 'tensor'), as said below
- w_value: bfloat16 [2048, 512], P('seq', 'tensor'), may hold values from -0.125 to 0.125
- w_out: bfloat16 [2048, 2048], P('tensor', 'seq'), may hold values from -0.125 to 0.125
- mlp_gain: float32 [2048], replicated, may hold values from 0.1 to 1.9
- w_gate: bfloat16 [2048, 5632], P('seq', 'tensor'), may hold values from -0.125 to 0.125
- w_up: bfloat16 [2048, 5632], P('seq', 'tensor'), may hold values from -0.125 to 0.125
- w_down: bfloat16 [5632, 2048], P('tensor', 'seq'), may hold values from -0.078125 to 0.078125
Outputs:
- layer_out: bfloat16 [4096, 2048], P('seq', 'tensor')
Inputs may be any that keep to these rules, and one draw needn't show every extreme that they name: `w_query`: entries are of order 2048 to the power -1/2. `w_key`: entries are of order 2048 to the power -1/2.
All inputs are finite; a program needn't handle non-finite values.
Results may differ from a plain program's by a relative error of at most 0.013.
Values may be sent and summed in bfloat16 or wider, within the bound.
A program may use at most 128 MiB of HBM per device.

v0:
```python
import jax
import jax.numpy as jnp
from jax import lax
from jax.sharding import PartitionSpec as P

HEAD_DIM = 128
WINDOW = 1024


def passed_along(block, axis, distance):
    devices = range(lax.axis_size(axis))
    route = [(i - distance, i) for i in devices if i - distance in devices]
    return lax.ppermute(block, axis, route)


def scaled_rows(values, gain):
    values = values.astype(jnp.float32)
    mean_square = jnp.mean(values * values, axis=1, keepdims=True)
    return (values * lax.rsqrt(mean_square + 1e-06) * gain).astype(jnp.bfloat16)


def product(left, right):
    return jnp.dot(left, right, preferred_element_type=jnp.float32)


def window_attention(queries, context_keys, context_values, reach, position):
    rows = queries.shape[0]
    local_kv = context_keys.shape[1] // HEAD_DIM
    group = queries.shape[1] // (local_kv * HEAD_DIM)
    block = min(512, rows)
    span = WINDOW + block
    scale = HEAD_DIM ** (-0.5)
    start = reach * rows - WINDOW
    query_block = queries.reshape(block, local_kv, group, HEAD_DIM)
    key_block = context_keys.reshape(span, local_kv, HEAD_DIM)
    value_block = context_values.reshape(span, local_kv, HEAD_DIM)
    scores = (
        jnp.einsum("qkgd,ckd->kgqc", query_block, key_block, preferred_element_type=jnp.float32)
        * scale
    )
    query_pos = lax.broadcasted_iota(jnp.int32, (block, span), 0)
    key_pos = lax.broadcasted_iota(jnp.int32, (block, span), 1)
    distance = query_pos + WINDOW - key_pos
    first_key = (position - reach) * rows + start
    allowed = (distance >= 0) & (distance < WINDOW) & (key_pos + first_key >= 0)
    scores = jnp.where(allowed[None, None], scores, -1e30)
    highest = jnp.max(scores, axis=3, keepdims=True)
    raised = jnp.exp(scores - highest)
    weights = (raised / jnp.sum(raised, axis=3, keepdims=True)).astype(jnp.bfloat16)
    mixed = jnp.einsum("kgqc,ckd->qkgd", weights, value_block, preferred_element_type=jnp.float32)
    outputs = mixed.astype(jnp.bfloat16).reshape(block, local_kv * group * HEAD_DIM)
    return outputs


def per_device(tokens, attn_gain, w_query, w_key, w_value, w_out, mlp_gain, w_gate, w_up, w_down):
    rows = tokens.shape[0]
    whole = lax.all_gather(tokens, "tensor", axis=1, tiled=True)
    normed = scaled_rows(whole, attn_gain)
    query_full = lax.all_gather(w_query, "seq", axis=0, tiled=True)
    key_full, value_full = (
        lax.all_gather(w_key, "seq", axis=0, tiled=True),
        lax.all_gather(w_value, "seq", axis=0, tiled=True),
    )
    queries = product(normed, query_full).astype(jnp.bfloat16)
    keys = product(normed, key_full).astype(jnp.bfloat16)
    values = product(normed, value_full).astype(jnp.bfloat16)
    reach = -(-WINDOW // rows)
    earlier = []
    for step in range(reach):
        earlier.append(passed_along((keys, values), "seq", step + 1))
    context_keys = jnp.concatenate(
        [earlier[reach - 1 - step][0] for step in range(reach)] + [keys], axis=0
    )
    context_values = jnp.concatenate(
        [earlier[reach - 1 - step][1] for step in range(reach)] + [values], axis=0
    )
    position = lax.axis_index("seq")
    attended = window_attention(queries, context_keys, context_values, reach, position)
    out_full = lax.all_gather(w_out, "seq", axis=1, tiled=True)
    head_terms = product(attended, out_full)
    share = tokens.shape[1]
    attn_whole = lax.psum(head_terms.astype(jnp.bfloat16), "tensor").astype(jnp.float32)
    stream_whole = (whole.astype(jnp.float32) + attn_whole).astype(jnp.bfloat16)
    stream_share = lax.dynamic_slice_in_dim(
        stream_whole, lax.axis_index("tensor") * share, share, 1
    )
    stream_normed = scaled_rows(stream_whole, mlp_gain)
    gate_full = lax.all_gather(w_gate, "seq", axis=0, tiled=True)
    up_full = lax.all_gather(w_up, "seq", axis=0, tiled=True)
    gate = product(stream_normed, gate_full)
    upward = product(stream_normed, up_full)
    hidden = (jax.nn.silu(gate) * upward).astype(jnp.bfloat16)
    down_full = lax.all_gather(w_down, "seq", axis=1, tiled=True)
    unit_terms = product(hidden, down_full)
    mlp_share = lax.psum_scatter(
        unit_terms.astype(jnp.bfloat16), "tensor", scatter_dimension=1, tiled=True
    ).astype(jnp.float32)
    return (stream_share.astype(jnp.float32) + mlp_share).astype(jnp.bfloat16)


def solution(mesh):
    in_specs = (
        P("seq", "tensor"),
        P(),
        P("seq", "tensor"),
        P("seq", "tensor"),
        P("seq", "tensor"),
        P("tensor", "seq"),
        P(),
        P("seq", "tensor"),
        P("seq", "tensor"),
        P("tensor", "seq"),
    )
    out_specs = P("seq", "tensor")
    return jax.shard_map(
        per_device, mesh=mesh, in_specs=in_specs, out_specs=out_specs, check_vma=False
    )
```

profile of v0, /device:TPU:0, one launch (start us, length us, event | category | flops | bytes accessed | tf_op | source)
XLA Modules:
  0.0 529.0 jit_solution(15447656682437301794)
XLA Ops:
  6.5 0.7 all-gather.7.cloned.1.call-update
  7.3 0.0 all-gather.9.cloned.1.call-start
  7.3 0.7 all-gather.9.cloned.1.call-update
  8.0 0.0 all-gather.11.cloned.1.call-start
  8.1 0.7 all-gather.11.cloned.1.call-update
  8.7 0.0 all-reduce.2.cloned.1.call-start
  8.8 33.4 %all_gather.26 = bf16[2048,128]{1,0:T(8,128)(2,1)S(1)} all-gather(bf16[256,128]{1,0:T(8,128)(2,1)} %param.13), channel_id=1, replica_groups=mesh['seq'=8,'tensor'=4] {'seq'}, dimensions={0}, use_global_device_ids=true | all-gather | bytes 589824 | tf_op jit(solution)/shard_map/all_gather | solution.py:61
  42.2 35.2 %all_gather.25 = bf16[2048,128]{1,0:T(8,128)(2,1)} all-gather(bf16[256,128]{1,0:T(8,128)(2,1)} %param.14), channel_id=1, replica_groups=mesh['seq'=8,'tensor'=4] {'seq'}, dimensions={0}, use_global_device_ids=true | all-gather | bytes 589824 | tf_op jit(solution)/shard_map/all_gather | solution.py:62
  77.3 1.3 fusion.14
  78.6 0.0 all-gather.7.cloned.1.call-done
  78.7 2.2 fusion.7
  80.9 2.4 convolution_convert_fusion.3
  83.3 1.3 collective-permute-start.2
  84.6 4.3 collective-permute-start.3
  88.9 0.8 convolution_convert_fusion.4
  89.6 2.7 collective-permute-start
  92.4 2.7 collective-permute-start.1
  95.1 0.0 all-gather.9.cloned.1.call-done
  95.1 3.0 convolution_convert_fusion.2
  98.1 0.0 collective-permute-done.2
  98.1 0.0 collective-permute-done.3
  98.1 3.3 fusion.1
  101.4 2.8 fusion
  104.2 0.0 collective-permute-done
  104.2 0.0 collective-permute-done.1
  104.2 4.8 fusion.16
  109.0 33.7 %all-gather.11.cloned.1.call-done = bf16[512,2048]{1,0:T(8,128)(2,1)} async-done(((bf16[512,256]{1,0:T(8,128)(2,1)}), bf16[512,2048]{1,0:T(8,128)(2,1)}) %all-gather.11.cloned.1.call-update) | async-done | bytes 2097168 | tf_op jit(solution)/shard_map/all_gather | solution.py:79
  142.7 4.4 convolution_convert_fusion
  147.1 0.0 all-reduce.2.cloned.1.call-update
  147.1 0.0 copy-start.4
  147.1 0.0 all-gather.13.cloned.1.call-start
  147.2 0.5 all-gather.13.cloned.1.call-update
  147.7 0.0 all-gather.15.cloned.1.call-start
  147.8 0.5 all-gather.15.cloned.1.call-update
  148.3 0.0 all-gather.17.cloned.1.call-start
  148.4 0.7 all-gather.17.cloned.1.call-update
  149.1 0.3 reduce-scatter.2.cloned.1.call-start
  149.3 47.5 %all-reduce.2.cloned.1.call-done = bf16[512,2048]{1,0:T(8,128)(2,1)} async-done(((bf16[512,2048]{1,0:T(8,128)(2,1)}), bf16[512,2048]{1,0:T(8,128)(2,1)}) %all-reduce.2.cloned.1.call-update) | async-done | bytes 2097168 | tf_op jit(solution)/shard_map/psum | solution.py:82
  196.9 3.9 fusion.4
  200.8 90.5 %all-gather.13.cloned.1.call-done = bf16[2048,1408]{1,0:T(8,128)(2,1)} async-done(((bf16[256,1408]{1,0:T(8,128)(2,1)}), bf16[2048,1408]{1,0:T(8,128)(2,1)}) %all-gather.13.cloned.1.call-update) | async-done | bytes 5767184 | tf_op jit(solution)/shard_map/all_gather | solution.py:88
  291.3 8.4 %fusion.21 = f32[512,1408]{1,0:T(8,128)} fusion(bf16[2048,1408]{1,0:T(8,128)(2,1)} %all-gather.13.cloned.1.call-done, bf16[512,2048]{1,0:T(8,128)(2,1)} %get-tuple-element.6, f32[2048]{0:T(1024)S(1)} %copy-done.4, f32[512]{0:T(512)S(1)} %add_rsqrt_fusion), kind=kOutput, calls=%fused_computation.33 | convolution fusion | flops 2956984320 | bytes 10758144 | tf_op jit(solution)/shard_map/dot_general | solution.py:23
  299.7 84.1 %all-gather.15.cloned.1.call-done = bf16[2048,1408]{1,0:T(8,128)(2,1)} async-done(((bf16[256,1408]{1,0:T(8,128)(2,1)}), bf16[2048,1408]{1,0:T(8,128)(2,1)}) %all-gather.15.cloned.1.call-update) | async-done | bytes 5767184 | tf_op jit(solution)/shard_map/all_gather | solution.py:89
  383.9 93.4 %all-gather.17.cloned.1.call-done = bf16[1408,2048]{1,0:T(8,128)(2,1)} async-done(((bf16[1408,256]{1,0:T(8,128)(2,1)}), bf16[1408,2048]{1,0:T(8,128)(2,1)}) %all-gather.17.cloned.1.call-update) | async-done | bytes 5767184 | tf_op jit(solution)/shard_map/all_gather | solution.py:93
  477.2 0.0 copy-done.1
  477.2 13.4 %convolution_convert_fusion.1 = bf16[512,2048]{1,0:T(8,128)(2,1)} fusion(bf16[1408,2048]{1,0:T(8,128)(2,1)} %all-gather.17.cloned.1.call-done, bf16[2048,1408]{1,0:T(8,128)(2,1)} %all-gather.15.cloned.1.call-done, f32[512,1408]{1,0:T(8,128)} %fusion.21, bf16[512,2048]{1,0:T(8,128)(2,1)S(1)} %copy-done.1, f32[2048]{0:T(1024)S(1)} %copy-done.4, ...), kind=kOutput, calls=%fused_computation.27 | convolution fusion | flops 5915148288 | bytes 18622464 | tf_op jit(solution)/shard_map/dot_general | solution.py:23
  490.7 0.0 reduce-scatter.2.cloned.1.call-update
  490.7 29.5 %reduce-scatter.2.cloned.1.call-done = bf16[512,512]{1,0:T(8,128)(2,1)} async-done(((bf16[512,2048]{1,0:T(8,128)(2,1)}), bf16[512,512]{1,0:T(8,128)(2,1)}) %reduce-scatter.2.cloned.1.call-update) | async-done | bytes 524304 | tf_op jit(solution)/shard_map/reduce_scatter | solution.py:95
  520.2 2.0 add_convert_fusion
  (13 shorter events, 0.0 us)
Async XLA Ops:
  6.5 74.4 %copy-start.3 = (f32[2048]{0:T(1024)S(1)}, f32[2048]{0:T(1024)}, u32[]{:S(2)}) copy-start(f32[2048]{0:T(1024)} %param.11) | copy-start | bytes 24580
  6.5 72.1 %all-gather.7.cloned.1.call-start = ((), (), s32[]{:S(2)}) async-start(), calls=%async_computation.1 | async-start | bytes 2621440 | tf_op jit(solution)/shard_map/all_gather | solution.py:57
  7.3 87.8 %all-gather.9.cloned.1.call-start = ((), (), s32[]{:S(2)}) async-start(), calls=%async_computation.2 | async-start | bytes 2359296 | tf_op jit(solution)/shard_map/all_gather | solution.py:59
  8.0 134.7 %all-gather.11.cloned.1.call-start = ((), (), s32[]{:S(2)}) async-start(), calls=%async_computation.3 | async-start | bytes 2359296 | tf_op jit(solution)/shard_map/all_gather | solution.py:79
  8.7 188.1 %all-reduce.2.cloned.1.call-start = ((), (), s32[]{:S(2)}) async-start(), calls=%async_computation.4 | async-start | bytes 4194304 | tf_op jit(solution)/shard_map/psum | solution.py:82
  78.6 10.2 %copy-start = (bf16[512,2048]{1,0:T(8,128)(2,1)S(1)}, bf16[512,2048]{1,0:T(8,128)(2,1)}, u32[]{:S(2)}) copy-start(bf16[512,2048]{1,0:T(8,128)(2,1)} %all-gather.7.cloned.1.call-done) | copy-start | bytes 6291460
  78.7 10.2 %copy-start.2 = (bf16[2048,128]{1,0:T(8,128)(2,1)S(1)}, bf16[2048,128]{1,0:T(8,128)(2,1)}, u32[]{:S(2)}) copy-start(bf16[2048,128]{1,0:T(8,128)(2,1)} %all_gather.25) | copy-start | bytes 1572868
  83.3 14.8 %collective-permute-start.2 = (bf16[512,128]{1,0:T(8,128)(2,1)S(1)}, bf16[512,128]{1,0:T(8,128)(2,1)S(1)}, u32[]{:S(2)}, u32[]{:S(2)}) collective-permute-start(bf16[512,128]{1,0:T(8,128)(2,1)S(1)} %convolution_convert_fusion.3), channel_id=1, source_target_pairs={{0,8},{4,12},{8,16},{12,20},{16,24},{20,28},{1,9},{5,13},{9,17},{1... | collective-permute-start | bytes 393224 | tf_op jit(solution)/shard_map/ppermute | solution.py:13
  84.6 13.5 %collective-permute-start.3 = (bf16[512,128]{1,0:T(8,128)(2,1)S(1)}, bf16[512,128]{1,0:T(8,128)(2,1)}, u32[]{:S(2)}, u32[]{:S(2)}) collective-permute-start(bf16[512,128]{1,0:T(8,128)(2,1)S(1)} %convolution_convert_fusion.3), channel_id=1, source_target_pairs={{0,4},{4,8},{8,12},{12,16},{16,20},{20,24},{24,28},{1,5},{5,9},{9,... | collective-permute-start | bytes 393224 | tf_op jit(solution)/shard_map/ppermute | solution.py:13
  89.6 14.5 %collective-permute-start = (bf16[512,128]{1,0:T(8,128)(2,1)S(1)}, bf16[512,128]{1,0:T(8,128)(2,1)S(1)}, u32[]{:S(2)}, u32[]{:S(2)}) collective-permute-start(bf16[512,128]{1,0:T(8,128)(2,1)S(1)} %convolution_convert_fusion.4), channel_id=1, source_target_pairs={{0,8},{4,12},{8,16},{12,20},{16,24},{20,28},{1,9},{5,13},{9,17},{1... | collective-permute-start | bytes 393224 | tf_op jit(solution)/shard_map/ppermute | solution.py:13
  92.4 11.8 %collective-permute-start.1 = (bf16[512,128]{1,0:T(8,128)(2,1)S(1)}, bf16[512,128]{1,0:T(8,128)(2,1)S(1)}, u32[]{:S(2)}, u32[]{:S(2)}) collective-permute-start(bf16[512,128]{1,0:T(8,128)(2,1)S(1)} %convolution_convert_fusion.4), channel_id=1, source_target_pairs={{0,4},{4,8},{8,12},{12,16},{16,20},{20,24},{24,28},{1,5},{5,9},{9,... | collective-permute-start | bytes 393224 | tf_op jit(solution)/shard_map/ppermute | solution.py:13
  147.1 144.2 %copy-start.4 = (f32[2048]{0:T(1024)S(1)}, f32[2048]{0:T(1024)}, u32[]{:S(2)}) copy-start(f32[2048]{0:T(1024)} %param.16) | copy-start | bytes 24580
  147.1 144.1 %all-gather.13.cloned.1.call-start = ((), (), s32[]{:S(2)}) async-start(), calls=%async_computation.5 | async-start | bytes 6488064 | tf_op jit(solution)/shard_map/all_gather | solution.py:88
  147.7 236.1 %all-gather.15.cloned.1.call-start = ((), (), s32[]{:S(2)}) async-start(), calls=%async_computation.6 | async-start | bytes 6488064 | tf_op jit(solution)/shard_map/all_gather | solution.py:89
  148.3 328.9 %all-gather.17.cloned.1.call-start = ((), (), s32[]{:S(2)}) async-start(), calls=%async_computation.7 | async-start | bytes 6488064 | tf_op jit(solution)/shard_map/all_gather | solution.py:93
  149.1 371.1 %reduce-scatter.2.cloned.1.call-start = ((), (), s32[]{:S(2)}) async-start(), calls=%async_computation.8 | async-start | bytes 2621440 | tf_op jit(solution)/shard_map/reduce_scatter | solution.py:95
  291.3 185.9 %copy-start.1 = (bf16[512,2048]{1,0:T(8,128)(2,1)S(1)}, bf16[512,2048]{1,0:T(8,128)(2,1)}, u32[]{:S(2)}) copy-start(bf16[512,2048]{1,0:T(8,128)(2,1)} %get-tuple-element.6) | copy-start | bytes 6291460
Sparse Core Ops, SparseCore 0:
  8.9 25.2 all-gather.6
  36.3 52.5 all-gather.8
  91.0 51.7 all-gather.10
  147.3 49.5 all-reduce.1
  198.9 92.3 all-gather.12
  293.3 90.4 all-gather.14
  385.9 91.2 all-gather.16
  490.8 29.3 reduce-scatter.1
where the time goes:
time: 529 us
  waiting for transfers between devices  383 us (72%)
  blocking collectives  68.5 us (13%)
  matrix products  40.5 us (8%)
  between operations  13.7 us (3%)
  other arithmetic  12.2 us (2%)
  starting transfers between devices  11.5 us (2%)
    all_gather x1, waiting for transfers between devices, per_device(): down_full = lax.all_gather(w_down, 'seq', axis=1, tiled=True)  93.4 us
    all_gather x1, waiting for transfers between devices, per_device(): gate_full = lax.all_gather(w_gate, 'seq', axis=0, tiled=True)  90.5 us
    all_gather x1, waiting for transfers between devices, per_device(): up_full = lax.all_gather(w_up, 'seq', axis=0, tiled=True)  84.1 us
    psum x1, waiting for transfers between devices, per_device(): lax.psum(head_terms.astype(jnp.bfloat16), 'tensor').astype(jnp.float32)  47.5 us
    all_gather x1, blocking collectives, per_device(): lax.all_gather(w_value, 'seq', axis=0, tiled=True)  35.2 us
    all_gather x1, waiting for transfers between devices, per_device(): out_full = lax.all_gather(w_out, 'seq', axis=1, tiled=True)  33.7 us
    all_gather x1, blocking collectives, per_device(): lax.all_gather(w_key, 'seq', axis=0, tiled=True)  33.4 us
    dot_general x6, matrix products, product(): return jnp.dot(left, right, preferred_element_type=jnp.float32)  32.3 us
  transfers between devices with their start and end apart: 12, of which 6 were waited for; matrix products, arithmetic and copies ran while one was open for 6% of the time, Pallas kernels for 0%

commit v1 on v0

--- a/solution.py
+++ b/solution.py
@@ -90,7 +90,8 @@
     gate = product(stream_normed, gate_full)
     upward = product(stream_normed, up_full)
     hidden = (jax.nn.silu(gate) * upward).astype(jnp.bfloat16)
-    down_full = lax.all_gather(w_down, "seq", axis=1, tiled=True)
+    parts = lax.all_gather(w_down, "seq", axis=0, tiled=False)
+    down_full = jnp.concatenate(parts, axis=1)
     unit_terms = product(hidden, down_full)
     mlp_share = lax.psum_scatter(
         unit_terms.astype(jnp.bfloat16), "tensor", scatter_dimension=1, tiled=True

time: 529 us -> 529 us (level)
  waiting for transfers between devices: 383 us -> 374 us
  local copies, waits for them, and re-layouts: 0.02 us -> 8.38 us
    reshape x0 -> x1, local copies, waits for them, and re-layouts: none -> 8.36 us  [per_device(): down_full = jnp.concatenate(parts, axis=1)]
    all_gather x1, waiting for transfers between devices: 90.5 us -> 84.2 us  [per_device(): gate_full = lax.all_gather(w_gate, 'seq', axis=0, tiled=True)]
  transfers between devices with their start and end apart: 12 -> 12, of which waited for: 6 -> 6; matrix products, arithmetic and copies ran while one was open for 6% -> 8% of each run, Pallas kernels for 0% -> 0%
where the time goes in v1:
time: 529 us; the launch traced here: 528 us
  waiting for transfers between devices  374 us (71%)
  blocking collectives  68.5 us (13%)
  matrix products  39.6 us (7%)
  between operations  13.6 us (3%)
  other arithmetic  12.2 us (2%)
  starting transfers between devices  11.5 us (2%)
  local copies, waits for them, and re-layouts  8.38 us (2%)
    all_gather x1, waiting for transfers between devices, per_device(): parts = lax.all_gather(w_down, 'seq', axis=0, tiled=False)  90.5 us
    all_gather x1, waiting for transfers between devices, per_device(): up_full = lax.all_gather(w_up, 'seq', axis=0, tiled=True)  85 us
    all_gather x1, waiting for transfers between devices, per_device(): gate_full = lax.all_gather(w_gate, 'seq', axis=0, tiled=True)  84.2 us
    psum x1, waiting for transfers between devices, per_device(): lax.psum(head_terms.astype(jnp.bfloat16), 'tensor').astype(jnp.float32)  47.5 us
    all_gather x1, blocking collectives, per_device(): lax.all_gather(w_value, 'seq', axis=0, tiled=True)  35.2 us
    all_gather x1, waiting for transfers between devices, per_device(): out_full = lax.all_gather(w_out, 'seq', axis=1, tiled=True)  33.7 us
    all_gather x1, blocking collectives, per_device(): lax.all_gather(w_key, 'seq', axis=0, tiled=True)  33.4 us
    dot_general x6, matrix products, product(): return jnp.dot(left, right, preferred_element_type=jnp.float32)  31.5 us
  transfers between devices with their start and end apart: 12, of which 6 were waited for; matrix products, arithmetic and copies ran while one was open for 8% of the time, Pallas kernels for 0%

profile of v1, /device:TPU:0, one launch (start us, length us, event | category | flops | bytes accessed | tf_op | source)
XLA Modules:
  0.0 528.2 jit_solution(10851936127894093240)
XLA Ops:
  6.5 0.7 all-gather.8.cloned.1.call-update
  7.3 0.0 all-gather.10.cloned.1.call-start
  7.3 0.7 all-gather.10.cloned.1.call-update
  8.0 0.0 all-gather.12.cloned.1.call-start
  8.1 0.7 all-gather.12.cloned.1.call-update
  8.7 0.0 all-reduce.2.cloned.1.call-start
  8.8 33.4 %all_gather.29 = bf16[2048,128]{1,0:T(8,128)(2,1)S(1)} all-gather(bf16[256,128]{1,0:T(8,128)(2,1)} %param.13), channel_id=1, replica_groups=mesh['seq'=8,'tensor'=4] {'seq'}, dimensions={0}, use_global_device_ids=true | all-gather | bytes 589824 | tf_op jit(solution)/shard_map/all_gather | solution.py:61
  42.2 35.2 %all_gather.28 = bf16[2048,128]{1,0:T(8,128)(2,1)} all-gather(bf16[256,128]{1,0:T(8,128)(2,1)} %param.14), channel_id=1, replica_groups=mesh['seq'=8,'tensor'=4] {'seq'}, dimensions={0}, use_global_device_ids=true | all-gather | bytes 589824 | tf_op jit(solution)/shard_map/all_gather | solution.py:62
  77.3 1.3 fusion.14
  78.6 0.0 all-gather.8.cloned.1.call-done
  78.7 2.2 fusion.7
  80.9 2.4 convolution_convert_fusion.3
  83.3 1.3 collective-permute-start.2
  84.6 4.3 collective-permute-start.3
  88.9 0.8 convolution_convert_fusion.4
  89.6 2.7 collective-permute-start
  92.4 2.7 collective-permute-start.1
  95.1 0.0 all-gather.10.cloned.1.call-done
  95.1 3.0 convolution_convert_fusion.2
  98.1 0.0 collective-permute-done.2
  98.1 0.0 collective-permute-done.3
  98.1 3.3 fusion.1
  101.4 2.8 fusion
  104.2 0.0 collective-permute-done
  104.2 0.0 collective-permute-done.1
  104.2 4.8 fusion.16
  109.0 33.7 %all-gather.12.cloned.1.call-done = bf16[512,2048]{1,0:T(8,128)(2,1)} async-done(((bf16[512,256]{1,0:T(8,128)(2,1)}), bf16[512,2048]{1,0:T(8,128)(2,1)}) %all-gather.12.cloned.1.call-update) | async-done | bytes 2097168 | tf_op jit(solution)/shard_map/all_gather | solution.py:79
  142.7 4.4 convolution_convert_fusion
  147.1 0.0 all-reduce.2.cloned.1.call-update
  147.1 0.0 all-gather.18.cloned.1.call-start
  147.2 0.5 all-gather.18.cloned.1.call-update
  147.7 0.0 all-gather.14.cloned.1.call-start
  147.8 0.5 all-gather.14.cloned.1.call-update
  148.3 0.0 all-gather.16.cloned.1.call-start
  148.3 0.7 all-gather.16.cloned.1.call-update
  149.1 0.3 reduce-scatter.2.cloned.1.call-start
  149.3 47.5 %all-reduce.2.cloned.1.call-done = bf16[512,2048]{1,0:T(8,128)(2,1)} async-done(((bf16[512,2048]{1,0:T(8,128)(2,1)}), bf16[512,2048]{1,0:T(8,128)(2,1)}) %all-reduce.2.cloned.1.call-update) | async-done | bytes 2097168 | tf_op jit(solution)/shard_map/psum | solution.py:82
  196.9 3.9 fusion.4
  200.8 90.5 %all-gather.18.cloned.1.call-done = bf16[11264,256]{1,0:T(8,128)(2,1)} async-done(((bf16[1408,256]{1,0:T(8,128)(2,1)}), bf16[11264,256]{1,0:T(8,128)(2,1)}) %all-gather.18.cloned.1.call-update) | async-done | bytes 5767184 | tf_op jit(solution)/shard_map/all_gather | solution.py:93
  291.3 8.4 %copy.20 = bf16[1408,8,256]{0,2,1:T(8,128)(2,1)} copy(bf16[1408,8,256]{2,0,1:T(8,128)(2,1)} %bitcast.47) | data formatting | bytes 11534336 | tf_op jit(solution)/shard_map/reshape | solution.py:94
  299.7 84.2 %all-gather.14.cloned.1.call-done = bf16[2048,1408]{1,0:T(8,128)(2,1)} async-done(((bf16[256,1408]{1,0:T(8,128)(2,1)}), bf16[2048,1408]{1,0:T(8,128)(2,1)}) %all-gather.14.cloned.1.call-update) | async-done | bytes 5767184 | tf_op jit(solution)/shard_map/all_gather | solution.py:88
  383.9 0.0 copy-done.1
  383.9 7.7 %fusion.21 = f32[512,1408]{1,0:T(8,128)} fusion(bf16[2048,1408]{1,0:T(8,128)(2,1)} %all-gather.14.cloned.1.call-done, bf16[512,2048]{1,0:T(8,128)(2,1)S(1)} %copy-done.1, f32[2048]{0:T(1024)S(1)} %copy-done.4, f32[512]{0:T(512)S(1)} %add_rsqrt_fusion), kind=kOutput, calls=%fused_computation.33 | convolution fusion | flops 2956984320 | bytes 10758144 | tf_op jit(solution)/shard_map/dot_general | solution.py:23
  391.6 85.0 %all-gather.16.cloned.1.call-done = bf16[2048,1408]{1,0:T(8,128)(2,1)} async-done(((bf16[256,1408]{1,0:T(8,128)(2,1)}), bf16[2048,1408]{1,0:T(8,128)(2,1)}) %all-gather.16.cloned.1.call-update) | async-done | bytes 5767184 | tf_op jit(solution)/shard_map/all_gather | solution.py:89
  476.6 13.3 %convolution_convert_fusion.1 = bf16[512,2048]{1,0:T(8,128)(2,1)} fusion(bf16[1408,2048]{0,1:T(8,128)(2,1)} %bitcast.48, bf16[2048,1408]{1,0:T(8,128)(2,1)} %all-gather.16.cloned.1.call-done, f32[512,1408]{1,0:T(8,128)} %fusion.21, bf16[512,2048]{1,0:T(8,128)(2,1)S(1)} %copy-done.1, f32[2048]{0:T(1024)S(1)} %copy-done.4, f32[512]{0:T(512)S(1)} %add_rsqrt_fusion), kind=kOutput, calls=%fused_computation.27 | convolution fusion | flops 5915148288 | bytes 18622464 | tf_op jit(solution)/shard_map/dot_general | solution.py:23
  489.8 0.0 reduce-scatter.2.cloned.1.call-update
  489.9 29.5 %reduce-scatter.2.cloned.1.call-done = bf16[512,512]{1,0:T(8,128)(2,1)} async-done(((bf16[512,2048]{1,0:T(8,128)(2,1)}), bf16[512,512]{1,0:T(8,128)(2,1)}) %reduce-scatter.2.cloned.1.call-update) | async-done | bytes 524304 | tf_op jit(solution)/shard_map/reduce_scatter | solution.py:96
  519.3 2.0 add_convert_fusion
  (14 shorter events, 0.0 us)
Async XLA Ops:
  6.5 74.4 %copy-start.3 = (f32[2048]{0:T(1024)S(1)}, f32[2048]{0:T(1024)}, u32[]{:S(2)}) copy-start(f32[2048]{0:T(1024)} %param.11) | copy-start | bytes 24580
  6.5 72.1 %all-gather.8.cloned.1.call-start = ((), (), s32[]{:S(2)}) async-start(), calls=%async_computation.1 | async-start | bytes 2621440 | tf_op jit(solution)/shard_map/all_gather | solution.py:57
  7.3 87.8 %all-gather.10.cloned.1.call-start = ((), (), s32[]{:S(2)}) async-start(), calls=%async_computation.2 | async-start | bytes 2359296 | tf_op jit(solution)/shard_map/all_gather | solution.py:59
  8.0 134.7 %all-gather.12.cloned.1.call-start = ((), (), s32[]{:S(2)}) async-start(), calls=%async_computation.3 | async-start | bytes 2359296 | tf_op jit(solution)/shard_map/all_gather | solution.py:79
  8.7 188.1 %all-reduce.2.cloned.1.call-start = ((), (), s32[]{:S(2)}) async-start(), calls=%async_computation.4 | async-start | bytes 4194304 | tf_op jit(solution)/shard_map/psum | solution.py:82
  78.6 10.2 %copy-start = (bf16[512,2048]{1,0:T(8,128)(2,1)S(1)}, bf16[512,2048]{1,0:T(8,128)(2,1)}, u32[]{:S(2)}) copy-start(bf16[512,2048]{1,0:T(8,128)(2,1)} %all-gather.8.cloned.1.call-done) | copy-start | bytes 6291460
  78.7 10.2 %copy-start.2 = (bf16[2048,128]{1,0:T(8,128)(2,1)S(1)}, bf16[2048,128]{1,0:T(8,128)(2,1)}, u32[]{:S(2)}) copy-start(bf16[2048,128]{1,0:T(8,128)(2,1)} %all_gather.28) | copy-start | bytes 1572868
  83.3 14.8 %collective-permute-start.2 = (bf16[512,128]{1,0:T(8,128)(2,1)S(1)}, bf16[512,128]{1,0:T(8,128)(2,1)S(1)}, u32[]{:S(2)}, u32[]{:S(2)}) collective-permute-start(bf16[512,128]{1,0:T(8,128)(2,1)S(1)} %convolution_convert_fusion.3), channel_id=1, source_target_pairs={{0,8},{4,12},{8,16},{12,20},{16,24},{20,28},{1,9},{5,13},{9,17},{1... | collective-permute-start | bytes 393224 | tf_op jit(solution)/shard_map/ppermute | solution.py:13
  84.6 13.5 %collective-permute-start.3 = (bf16[512,128]{1,0:T(8,128)(2,1)S(1)}, bf16[512,128]{1,0:T(8,128)(2,1)}, u32[]{:S(2)}, u32[]{:S(2)}) collective-permute-start(bf16[512,128]{1,0:T(8,128)(2,1)S(1)} %convolution_convert_fusion.3), channel_id=1, source_target_pairs={{0,4},{4,8},{8,12},{12,16},{16,20},{20,24},{24,28},{1,5},{5,9},{9,... | collective-permute-start | bytes 393224 | tf_op jit(solution)/shard_map/ppermute | solution.py:13
  89.6 14.5 %collective-permute-start = (bf16[512,128]{1,0:T(8,128)(2,1)S(1)}, bf16[512,128]{1,0:T(8,128)(2,1)S(1)}, u32[]{:S(2)}, u32[]{:S(2)}) collective-permute-start(bf16[512,128]{1,0:T(8,128)(2,1)S(1)} %convolution_convert_fusion.4), channel_id=1, source_target_pairs={{0,8},{4,12},{8,16},{12,20},{16,24},{20,28},{1,9},{5,13},{9,17},{1... | collective-permute-start | bytes 393224 | tf_op jit(solution)/shard_map/ppermute | solution.py:13
  92.4 11.8 %collective-permute-start.1 = (bf16[512,128]{1,0:T(8,128)(2,1)S(1)}, bf16[512,128]{1,0:T(8,128)(2,1)S(1)}, u32[]{:S(2)}, u32[]{:S(2)}) collective-permute-start(bf16[512,128]{1,0:T(8,128)(2,1)S(1)} %convolution_convert_fusion.4), channel_id=1, source_target_pairs={{0,4},{4,8},{8,12},{12,16},{16,20},{20,24},{24,28},{1,5},{5,9},{9,... | collective-permute-start | bytes 393224 | tf_op jit(solution)/shard_map/ppermute | solution.py:13
  147.1 144.2 %all-gather.18.cloned.1.call-start = ((), (), s32[]{:S(2)}) async-start(), calls=%async_computation.8 | async-start | bytes 6488064 | tf_op jit(solution)/shard_map/all_gather | solution.py:93
  147.7 236.1 %all-gather.14.cloned.1.call-start = ((), (), s32[]{:S(2)}) async-start(), calls=%async_computation.5 | async-start | bytes 6488064 | tf_op jit(solution)/shard_map/all_gather | solution.py:88
  148.3 328.3 %all-gather.16.cloned.1.call-start = ((), (), s32[]{:S(2)}) async-start(), calls=%async_computation.6 | async-start | bytes 6488064 | tf_op jit(solution)/shard_map/all_gather | solution.py:89
  149.1 370.3 %reduce-scatter.2.cloned.1.call-start = ((), (), s32[]{:S(2)}) async-start(), calls=%async_computation.7 | async-start | bytes 2621440 | tf_op jit(solution)/shard_map/reduce_scatter | solution.py:96
  291.3 92.6 %copy-start.1 = (bf16[512,2048]{1,0:T(8,128)(2,1)S(1)}, bf16[512,2048]{1,0:T(8,128)(2,1)}, u32[]{:S(2)}) copy-start(bf16[512,2048]{1,0:T(8,128)(2,1)} %get-tuple-element.6) | copy-start | bytes 6291460
  291.3 92.6 %copy-start.4 = (f32[2048]{0:T(1024)S(1)}, f32[2048]{0:T(1024)}, u32[]{:S(2)}) copy-start(f32[2048]{0:T(1024)} %param.16) | copy-start | bytes 24580
Sparse Core Ops, SparseCore 0:
  8.9 25.2 all-gather.7
  36.3 52.5 all-gather.9
  91.0 51.7 all-gather.11
  147.3 49.5 all-reduce.1
  198.9 92.3 all-gather.17
  293.3 90.4 all-gather.13
  386.0 90.4 all-gather.15
  490.0 29.3 reduce-scatter.1
